TPU v7x, 32 devices: a whole 2x2x4 slice. The times are simulated.
32 devices in a mesh: shot: 2 (over x), mp: 16 (over z, y, core).
Axes of the slice: x: 2, y: 2, z: 4, core: 2. Of those that a mesh axis runs over, the one named last changes fastest.
Arguments:
- gradient_parts: float32 [8, 1024, 1024], P('shot', 'mp')
- history_s: bfloat16 [10, 1024, 1024], P(None, 'mp'), may hold values from -6 to 6
- history_y: bfloat16 [10, 1024, 1024], P(None, 'mp'), as said below
Outputs:
- direction: float32 [1024, 1024], P('mp', 'shot')
Inputs may be any that keep to these rules, and one draw needn't show every extreme that they name: In every cell, history_y[i] equals history_s[i] times a factor between 0.5 and 4.
All inputs are finite; a program needn't handle non-finite values.
Results may differ from a plain program's by a relative error of at most 0.0003.
Values sent between devices are 32-bit elements; how exact they have to be, the bound alone decides.
A program may use at most 64 MiB of HBM per device.

v0:
```python
import jax
import jax.numpy as jnp
from jax import lax
from jax.sharding import PartitionSpec as P

M = 10


def from_gram(gradient, steps, changes):
    shape = gradient.shape
    flat_grad = gradient.reshape(-1)
    stacked = jnp.concatenate([steps.reshape(M, -1), changes.reshape(M, -1)], axis=0)
    hist_gram = lax.dot_general(
        stacked, stacked, (((1,), (1,)), ((), ())), preferred_element_type=jnp.float32
    )
    stacked_wide = stacked.astype(jnp.float32)
    cross = jnp.dot(stacked_wide, flat_grad, precision=lax.Precision.HIGHEST)
    grad_sq = jnp.sum(flat_grad * flat_grad)
    top = jnp.concatenate([hist_gram, cross[:, None]], axis=1)
    bottom = jnp.concatenate([cross, grad_sq[None]])[None, :]
    gram = lax.psum(jnp.concatenate([top, bottom], axis=0), ("shot", "mp"))
    coeffs = jnp.zeros((2 * M + 1,), jnp.float32).at[2 * M].set(1.0)
    alphas = [None] * M
    for i in reversed(range(M)):
        rho_i = 1.0 / gram[i, M + i]
        alphas[i] = rho_i * jnp.dot(gram[i], coeffs, precision=lax.Precision.HIGHEST)
        coeffs = coeffs.at[M + i].add(-alphas[i])
    coeffs = coeffs * (gram[M - 1, 2 * M - 1] / gram[2 * M - 1, 2 * M - 1])
    for i in range(M):
        rho_i = 1.0 / gram[i, M + i]
        beta = rho_i * jnp.dot(gram[M + i], coeffs, precision=lax.Precision.HIGHEST)
        coeffs = coeffs.at[i].add(alphas[i] - beta)
    combined = (
        jnp.dot(coeffs[: 2 * M], stacked_wide, precision=lax.Precision.HIGHEST)
        + coeffs[2 * M] * flat_grad
    )
    return -combined.reshape(shape)


def shards(gradient_parts, history_s, history_y):
    partial_grad = jnp.sum(gradient_parts, axis=0)
    columns = partial_grad.shape[1] // lax.axis_size("shot")
    start = lax.axis_index("shot") * columns
    gradient = lax.psum_scatter(partial_grad, "shot", scatter_dimension=1, tiled=True)
    steps = lax.dynamic_slice_in_dim(history_s, start, columns, 2)
    changes = lax.dynamic_slice_in_dim(history_y, start, columns, 2)
    result = from_gram(gradient, steps, changes)
    return result


def solution(mesh):
    placed = (P("shot", "mp", None), P(None, "mp", None), P(None, "mp", None))
    return jax.shard_map(
        shards, mesh=mesh, in_specs=placed, out_specs=P("mp", "shot"), check_vma=False
    )
```

profile of v0, /device:TPU:0, one launch (start us, length us, event | category | flops | bytes accessed | tf_op | source)
XLA Modules:
  0.0 115.3 jit_solution(11096996644224984904)
XLA Ops:
  6.5 2.1 %reduce_sum.18 = f32[64,1024]{1,0:T(8,128)} reduce(f32[4,64,1024]{2,1,0:T(8,128)} %param.45, f32[]{:T(128)} %constant.493.clone.1), dimensions={0}, to_apply=%region_0.0 | reduce | flops 196608 | bytes 1310724 | tf_op jit(solution)/shard_map/reduce_sum | solution.py:41
  8.7 1.2 %constant_dynamic-slice_fusion = (bf16[10,64,512]{2,1,0:T(8,128)(2,1)S(1)}, bf16[10,64,512]{2,1,0:T(8,128)(2,1)S(1)}) fusion(bf16[10,64,1024]{2,1,0:T(8,128)(2,1)S(1)} %copy-done.1, s32[]{:T(128)S(6)} %select_n.4, bf16[10,64,1024]{2,1,0:T(8,128)(2,1)} %param.46), kind=kLoop, calls=%fused_computation.25 | loop fusion | bytes 2621444 | tf_op jit(solution)/shard_map/dynamic_slice | solution.py:46
  11.3 0.9 fusion.4
  12.2 11.9 %reduce-scatter.2.cloned.1.call-done = f32[64,512]{1,0:T(8,128)} async-done(((f32[64,1024]{1,0:T(8,128)}), f32[64,512]{1,0:T(8,128)}) %reduce-scatter.2.cloned.1.call-update) | async-done | bytes 131088 | tf_op jit(solution)/shard_map/reduce_scatter | solution.py:44
  24.1 1.1 copy.49
  25.2 1.7 %fusion.3 = f32[1,20]{1,0:T(1,128)S(1)} fusion(f32[32768,1]{0,1:T(1,128)S(1)} %bitcast.66, bf16[10,32768]{1,0:T(8,128)(2,1)S(1)} %bitcast.62, bf16[10,32768]{1,0:T(8,128)(2,1)S(1)} %bitcast.59), kind=kOutput, calls=%fused_computation.71 | convolution fusion | flops 10485760 | bytes 1441872 | tf_op jit(solution)/shard_map/dot_general | solution.py:17
  26.9 0.7 multiply_reduce_fusion
  27.6 0.7 maximum_bitcast_fusion
  28.5 39.4 %psum.7 = f32[21,21]{0,1:T(8,128)S(1)} all-reduce(f32[21,21]{0,1:T(8,128)S(1)} %pad_maximum_fusion.1), channel_id=1, replica_groups=mesh['shot'=2,'mp'=16] {'shot','mp'}, use_global_device_ids=true, to_apply=%region_3.0 | all-reduce | flops 441 | bytes 3528 | tf_op jit(solution)/shard_map/psum | solution.py:21
  67.9 0.7 fusion.5
  71.8 0.7 multiply_reduce_fusion.19
  77.8 0.7 multiply_reduce_fusion.16
  79.9 0.6 multiply_reduce_fusion.15
  82.1 0.7 multiply_reduce_fusion.14
  84.3 0.7 multiply_reduce_fusion.13
  86.5 0.6 multiply_reduce_fusion.12
  88.5 0.6 multiply_reduce_fusion.11
  91.3 0.6 multiply_reduce_fusion.10
  92.6 0.6 multiply_reduce_fusion.9
  94.0 0.6 multiply_reduce_fusion.8
  95.4 0.6 multiply_reduce_fusion.7
  105.2 1.2 %fusion = f32[1,32768]{1,0:T(1,128)S(1)} fusion(f32[21]{0:T(128)S(1)} %constant_dynamic-update-slice_fusion.1, bf16[10,32768]{1,0:T(8,128)(2,1)S(1)} %bitcast.63, bf16[10,32768]{1,0:T(8,128)(2,1)S(1)} %bitcast.60), kind=kOutput, calls=%fused_computation.28 | convolution fusion | flops 10485760 | bytes 1441876 | tf_op jit(solution)/shard_map/dot_general | solution.py:34
  107.1 0.7 add_negate_fusion
  107.7 0.7 neg.47
  (48 shorter events, 11.1 us)
Async XLA Ops:
  6.5 2.1 %copy-start.1 = (bf16[10,64,1024]{2,1,0:T(8,128)(2,1)S(1)}, bf16[10,64,1024]{2,1,0:T(8,128)(2,1)}, u32[]{:S(2)}) copy-start(bf16[10,64,1024]{2,1,0:T(8,128)(2,1)} %param.47) | copy-start | bytes 3932164
  6.5 17.5 %reduce-scatter.2.cloned.1.call-start = ((), (), s32[]{:S(2)}) async-start(), calls=%async_computation.1 | async-start | bytes 393216 | tf_op jit(solution)/shard_map/reduce_scatter | solution.py:44
  10.7 0.7 copy-start.2
  24.1 2.9 %copy-start = (f32[64,512]{1,0:T(8,128)S(1)}, f32[64,512]{1,0:T(8,128)}, u32[]{:S(2)}) copy-start(f32[64,512]{1,0:T(8,128)} %reduce-scatter.2.cloned.1.call-done) | copy-start | bytes 393220
Sparse Core Ops, SparseCore 0:
  9.6 14.4 reduce-scatter.1
where the time goes:
time: 116 us; the launch traced here: 115 us
  blocking collectives  39.4 us (34%)
  between operations  34.3 us (30%)
  other arithmetic  19.3 us (17%)
  waiting for transfers between devices  11.9 us (10%)
  local copies, waits for them, and re-layouts  6.54 us (6%)
  matrix products  3.83 us (3%)
    psum x1, blocking collectives, from_gram(): gram = lax.psum(jnp.concatenate([top, bottom], axis=0), ('shot', 'mp'))  39.4 us
    reduce_scatter x1, waiting for transfers between devices, shards(): lax.psum_scatter(partial_grad, 'shot', scatter_dimension=1, tiled=True)  11.9 us
    dot_general x10, other arithmetic, from_gram(): jnp.dot(gram[i], coeffs, precision=lax.Precision.HIGHEST)  6.32 us
    dot_general x10, other arithmetic, from_gram(): beta = rho_i * jnp.dot(gram[M + i], coeffs, precision=lax.Precision.HIGHEST)  6.05 us
    unnamed x13, local copies, waits for them, and re-layouts  2.55 us
  transfers between devices with their start and end apart: 1, of which 1 were waited for; matrix products, arithmetic and copies ran while one was open for 3% of the time, Pallas kernels for 0%

commit v1 on v0

--- a/solution.py
+++ b/solution.py
@@ -18,7 +18,7 @@
     grad_sq = jnp.sum(flat_grad * flat_grad)
     top = jnp.concatenate([hist_gram, cross[:, None]], axis=1)
     bottom = jnp.concatenate([cross, grad_sq[None]])[None, :]
-    gram = lax.psum(jnp.concatenate([top, bottom], axis=0), ("shot", "mp"))
+    gram = lax.psum(lax.psum(jnp.concatenate([top, bottom], axis=0), "mp"), "shot")
     coeffs = jnp.zeros((2 * M + 1,), jnp.float32).at[2 * M].set(1.0)
     alphas = [None] * M
     for i in reversed(range(M)):

time: 116 us -> 145 us (1.25)
  blocking collectives: 39.4 us -> 68.1 us
    psum x1 -> x2, blocking collectives: 39.4 us -> 68.1 us  [the longest x1 61 us: from_gram(): lax.psum(jnp.concatenate([top, bottom], axis=0), 'mp')]
  transfers between devices with their start and end apart: 1 -> 1, of which waited for: 1 -> 1; matrix products, arithmetic and copies ran while one was open for 3% -> 2% of each run, Pallas kernels for 0% -> 0%
where the time goes in v1:
time: 145 us; the launch traced here: 144 us
  blocking collectives  68.1 us (47%)
  between operations  34.3 us (24%)
  other arithmetic  19.3 us (13%)
  waiting for transfers between devices  11.9 us (8%)
  local copies, waits for them, and re-layouts  6.54 us (5%)
  matrix products  3.83 us (3%)
    psum x1, blocking collectives, from_gram(): lax.psum(jnp.concatenate([top, bottom], axis=0), 'mp')  61 us
    reduce_scatter x1, waiting for transfers between devices, shards(): lax.psum_scatter(partial_grad, 'shot', scatter_dimension=1, tiled=True)  11.9 us
    psum x1, blocking collectives, from_gram(): lax.psum(lax.psum(jnp.concatenate([top, bottom], axis=0), 'mp'), 'shot')  7.11 us
    dot_general x10, other arithmetic, from_gram(): jnp.dot(gram[i], coeffs, precision=lax.Precision.HIGHEST)  6.32 us
    dot_general x10, other arithmetic, from_gram(): beta = rho_i * jnp.dot(gram[M + i], coeffs, precision=lax.Precision.HIGHEST)  6.05 us
  transfers between devices with their start and end apart: 1, of which 1 were waited for; matrix products, arithmetic and copies ran while one was open for 2% of the time, Pallas kernels for 0%

profile of v1, /device:TPU:0, one launch (start us, length us, event | category | flops | bytes accessed | tf_op | source)
XLA Modules:
  0.0 144.0 jit_solution(866326971893934489)
XLA Ops:
  6.5 2.1 %reduce_sum.18 = f32[64,1024]{1,0:T(8,128)} reduce(f32[4,64,1024]{2,1,0:T(8,128)} %param.45, f32[]{:T(128)} %constant.493.clone.1), dimensions={0}, to_apply=%region_0.0 | reduce | flops 196608 | bytes 1310724 | tf_op jit(solution)/shard_map/reduce_sum | solution.py:41
  8.7 1.2 constant_dynamic-slice_fusion
  11.3 0.9 fusion.4
  12.2 11.9 %reduce-scatter.2.cloned.1.call-done = f32[64,512]{1,0:T(8,128)} async-done(((f32[64,1024]{1,0:T(8,128)}), f32[64,512]{1,0:T(8,128)}) %reduce-scatter.2.cloned.1.call-update) | async-done | bytes 131088 | tf_op jit(solution)/shard_map/reduce_scatter | solution.py:44
  24.1 1.1 copy.49
  25.2 1.7 %fusion.3 = f32[1,20]{1,0:T(1,128)S(1)} fusion(f32[32768,1]{0,1:T(1,128)S(1)} %bitcast.66, bf16[10,32768]{1,0:T(8,128)(2,1)S(1)} %bitcast.62, bf16[10,32768]{1,0:T(8,128)(2,1)S(1)} %bitcast.59), kind=kOutput, calls=%fused_computation.71 | convolution fusion | flops 10485760 | bytes 1441872 | tf_op jit(solution)/shard_map/dot_general | solution.py:17
  26.9 0.7 multiply_reduce_fusion
  27.6 0.7 maximum_bitcast_fusion
  28.5 61.0 %psum.14 = f32[21,21]{0,1:T(8,128)S(1)} all-reduce(f32[21,21]{0,1:T(8,128)S(1)} %pad_maximum_fusion.1), channel_id=1, replica_groups=mesh['shot'=2,'mp'=16] {'mp'}, use_global_device_ids=true, to_apply=%region_3.0 | all-reduce | flops 441 | bytes 3528 | tf_op jit(solution)/shard_map/psum | solution.py:21
  89.5 7.1 %psum.15 = f32[21,21]{0,1:T(8,128)S(1)} all-reduce(f32[21,21]{0,1:T(8,128)S(1)} %psum.14), channel_id=1, replica_groups=mesh['shot'=2,'mp'=16] {'shot'}, use_global_device_ids=true, to_apply=%region_4.0 | all-reduce | flops 441 | bytes 3528 | tf_op jit(solution)/shard_map/psum | solution.py:21
  96.6 0.7 fusion.5
  100.6 0.7 multiply_reduce_fusion.19
  106.5 0.7 multiply_reduce_fusion.16
  108.7 0.6 multiply_reduce_fusion.15
  110.8 0.7 multiply_reduce_fusion.14
  113.0 0.7 multiply_reduce_fusion.13
  115.2 0.6 multiply_reduce_fusion.12
  117.3 0.6 multiply_reduce_fusion.11
  120.0 0.6 multiply_reduce_fusion.10
  121.3 0.6 multiply_reduce_fusion.9
  122.7 0.6 multiply_reduce_fusion.8
  134.0 1.2 fusion
  135.8 0.7 add_negate_fusion
  136.5 0.7 neg.47
  (49 shorter events, 11.7 us)
Async XLA Ops:
  6.5 2.1 %copy-start.1 = (bf16[10,64,1024]{2,1,0:T(8,128)(2,1)S(1)}, bf16[10,64,1024]{2,1,0:T(8,128)(2,1)}, u32[]{:S(2)}) copy-start(bf16[10,64,1024]{2,1,0:T(8,128)(2,1)} %param.47) | copy-start | bytes 3932164
  6.5 17.5 %reduce-scatter.2.cloned.1.call-start = ((), (), s32[]{:S(2)}) async-start(), calls=%async_computation.1 | async-start | bytes 393216 | tf_op jit(solution)/shard_map/reduce_scatter | solution.py:44
  10.7 0.7 copy-start.2
  24.1 2.9 %copy-start = (f32[64,512]{1,0:T(8,128)S(1)}, f32[64,512]{1,0:T(8,128)}, u32[]{:S(2)}) copy-start(f32[64,512]{1,0:T(8,128)} %reduce-scatter.2.cloned.1.call-done) | copy-start | bytes 393220
Sparse Core Ops, SparseCore 0:
  9.6 14.4 reduce-scatter.1
